TPU v7x, 512 devices: a whole 4x8x8 slice. The times are simulated.
512 devices in a mesh: row: 32 (over x, y), shift: 16 (over z, core).
Axes of the slice: x: 4, y: 8, z: 8, core: 2. Of those that a mesh axis runs over, the one named last changes fastest.
Arguments:
- snapshots: bfloat16 [4096, 2, 128], P('row'), may hold values from -6 to 6
- tail_sensors: bfloat16 [128, 2, 128], replicated, may hold values from -6 to 6
- shift_offsets: int32 [48], P('shift'), may hold values from 0 to 128
- start_basis: float32 [64, 4096], P(None, 'row'), may hold values from -0.09375 to 0.09375
Outputs:
- covariance: float32 [4096, 4096], P('row', 'shift')
- signal_basis: float32 [64, 4096], P(None, 'row')
Inputs may be any that keep to these rules, and one draw needn't show every extreme that they name: `shift_offsets`: each shift's first sensor.
All inputs are finite; a program needn't handle non-finite values.
Results may differ from a plain program's by a relative error of at most 0.0031.
Values may be sent and summed in bfloat16 or wider, within the bound.
No kernel may reach another device: no remote copies, remote signals or barrier semaphores. Data moves between devices by JAX's collectives and lax.ppermute only.
A program may use at most 64 MiB of HBM per device.

v0:
```python
import jax
import jax.numpy as jnp
from jax import lax
from jax.sharding import Mesh
from jax.sharding import PartitionSpec as P

M = 4096
SNAPS = 128
ITERS = 2
ROW = ("row_0", "row_1")


half_root = 0.7071067811865476


def joined_along(tiles, dim):
    tiles = jnp.moveaxis(tiles, 0, dim)
    lengths = tiles.shape
    return tiles.reshape(*lengths[:dim], lengths[dim] * lengths[dim + 1], *lengths[dim + 2 :])


def stacked_from(x, axes, order):
    tiles = x
    for k in order:
        tiles = lax.all_gather(tiles, axes[k])
    done = order[::-1]
    back = [done.index(k) for k in range(len(axes))]
    tiles = tiles.transpose(*back, *range(len(axes), tiles.ndim))
    return tiles.reshape(-1, *x.shape)


def whole_of(x, axes, order, dim):
    return joined_along(stacked_from(x, axes, order), dim)


def sent_to_all(x, axis):
    copies = jnp.broadcast_to(x, (lax.axis_size(axis), *x.shape))
    return lax.all_to_all(copies, axis, split_axis=0, concat_axis=0, tiled=True)


def gather_directly(x, axis, dim):
    tiles = sent_to_all(x, axis)
    return joined_along(tiles, dim)


def total_of_pieces(x, axis):
    tiles = lax.all_gather(x, axis)
    return tiles.sum(axis=0)


def make_some(extended, offset, start, count):
    window = lax.dynamic_slice_in_dim(extended, offset + start, count, 0).astype(jnp.float32)
    mirror = lax.dynamic_slice_in_dim(extended, offset + M - start - count, count, 0).astype(
        jnp.float32
    )[::-1]
    summed_pair = window + mirror
    difference = window - mirror
    upper_rows = jnp.concatenate([summed_pair[:, 0], summed_pair[:, 1]], axis=1)
    bottom = jnp.concatenate([difference[:, 1], -difference[:, 0]], axis=1)
    positions = start + jnp.arange(count, dtype=jnp.int32)
    chosen = jnp.where((positions < M // 2)[:, None], upper_rows, bottom)
    return (chosen * half_root).astype(jnp.bfloat16)


def factor(gram_matrix):
    lower_factor = jnp.linalg.cholesky(gram_matrix)
    identity = jnp.eye(gram_matrix.shape[0], dtype=jnp.float32)
    return jax.scipy.linalg.solve_triangular(lower_factor, identity, lower=True)


def per_device(snapshots, tail_sensors, shift_offsets, start_basis):
    block_rows = snapshots.shape[0]
    row_index = lax.axis_index(ROW)
    shift_index = lax.axis_index("shift")
    col_count = M // lax.axis_size("shift")
    normalizer = 1.0 / (SNAPS * shift_offsets.shape[0] * lax.axis_size("shift"))
    gathered = whole_of(snapshots, ROW, (0, 1), 0)
    extended = jnp.concatenate([gathered, tail_sensors], 0)
    every_offset = gather_directly(shift_offsets, "shift", 0)
    row_start = row_index * block_rows
    col_start = shift_index * col_count

    def add_block(which, running):
        offset = every_offset[which]
        own_rows = make_some(extended, offset, row_start, block_rows)
        col_rows = make_some(extended, offset, col_start, col_count)
        return running + lax.dot_general(
            own_rows, col_rows, (((1,), (1,)), ((), ())), preferred_element_type=jnp.float32
        )

    summed_block = lax.fori_loop(
        0, every_offset.shape[0], add_block, jnp.zeros((block_rows, col_count), jnp.float32)
    )
    cov_out = summed_block * normalizer
    basis_rows = gather_directly(start_basis, ROW, 1)
    own_basis = start_basis
    for sweep in range(ITERS):
        basis_cols = lax.dynamic_slice_in_dim(basis_rows, shift_index * col_count, col_count, 1)
        column_terms = lax.dot_general(
            basis_cols, cov_out, (((1,), (1,)), ((), ())), precision=lax.Precision.HIGHEST
        )
        mapped = total_of_pieces(column_terms, "shift")
        full_image = gather_directly(mapped, ROW, 1)
        gram_matrix = jnp.dot(full_image, full_image.T, precision=lax.Precision.HIGHEST)
        basis_rows = jnp.dot(factor(gram_matrix), full_image, precision=lax.Precision.HIGHEST)
        own_basis = lax.dynamic_slice_in_dim(basis_rows, row_index * block_rows, block_rows, 1)
    return (cov_out, own_basis)


def solution(mesh):
    split = Mesh(mesh.devices.reshape(4, 8, mesh.shape["shift"]), ("row_0", "row_1", "shift"))
    in_specs = (P(ROW, None, None), P(), P("shift"), P(None, ROW))
    out_specs = (P(ROW, "shift"), P(None, ROW))
    return jax.shard_map(
        per_device, mesh=split, in_specs=in_specs, out_specs=out_specs, check_vma=False
    )
```

profile of v0, /device:TPU:1, one launch (start us, length us, event | category | flops | bytes accessed | tf_op | source)
XLA Modules:
  0.0 395.8 jit_solution(15527877105455967366)
XLA Ops:
  7.2 0.9 copy.63
  8.1 11.3 %all-gather = bf16[512,2,128]{2,0,1:T(8,128)(2,1)} all-gather(bf16[128,2,128]{2,0,1:T(8,128)(2,1)S(1)} %copy.63), channel_id=2, replica_groups=mesh['row_0'=4,'row_1'=8,'shift'=16] {'row_0'}, dimensions={0}, use_global_device_ids=true | all-gather | bytes 327680 | tf_op jit(solution)/shard_map/all_gather | solution.py:25
  19.4 0.7 broadcast_in_dim.73
  20.0 20.7 %all_to_all.21 = s32[16,1,3]{2,1,0:T(1,128)S(1)} all-to-all(s32[16,1,3]{2,1,0:T(1,128)S(1)} %broadcast_in_dim.73), channel_id=1, replica_groups=mesh['row_0'=4,'row_1'=8,'shift'=16] {'shift'}, dimensions={0} | all-to-all | bytes 384 | tf_op jit(solution)/shard_map/all_to_all | solution.py:38
  40.8 1.9 broadcast_in_dim.74
  42.6 9.3 %all-to-all-start.1 = ((f32[32,64,128]{2,1,0:T(8,128)}), f32[32,64,128]{2,1,0:T(8,128)S(1)}, u32[]{:S(2)}, u32[]{:S(2)}) async-start(f32[32,64,128]{2,1,0:T(8,128)} %broadcast_in_dim.74), calls=%async_computation.1 | async-start | bytes 2097152 | tf_op jit(solution)/shard_map/all_to_all | solution.py:38
  52.5 0.7 reduce.7
  53.3 33.4 %all-to-all-done.1 = f32[32,64,128]{2,1,0:T(8,128)S(1)} async-done(((f32[32,64,128]{2,1,0:T(8,128)}), f32[32,64,128]{2,1,0:T(8,128)S(1)}, u32[]{:S(2)}, u32[]{:S(2)}) %all-to-all-start.1) | async-done | bytes 1048608 | tf_op jit(solution)/shard_map/all_to_all | solution.py:38
  86.6 1.1 copy_bitcast_fusion
  87.7 1.7 copy.65
  89.6 162.9 %while.18 = (s32[]{:T(128)}, f32[128,256]{1,0:T(8,128)S(1)}, s32[]{:T(128)}, s32[48]{0:T(128)S(1)}, bf16[4224,2,128]{2,0,1:T(8,128)(2,1)S(1)}, /*index=5*/s32[]{...) while((s32[]{:T(128)}, f32[128,256]{1,0:T(8,128)S(1)}, ...), condition=%wide.region_1.2_spmd.clone, body=%wide.region_0.1_spmd.clone.sunk | while | flops 17777428 | bytes 5375111 | solution.py:91
  89.6 0.6 dynamic_slice.102
  103.2 0.6 dynamic_slice.102
  116.7 0.6 dynamic_slice.102
  120.1 0.6 dynamic_slice.102
  133.7 0.6 dynamic_slice.102
  137.1 0.6 dynamic_slice.102
  150.7 0.6 dynamic_slice.102
  154.1 0.6 dynamic_slice.102
  167.6 0.6 dynamic_slice.102
  181.2 0.6 dynamic_slice.102
  184.6 0.6 dynamic_slice.102
  198.2 0.6 dynamic_slice.102
  201.6 0.6 dynamic_slice.102
  215.1 0.6 dynamic_slice.102
  218.5 0.6 dynamic_slice.102
  232.1 0.6 dynamic_slice.102
  245.7 0.6 dynamic_slice.102
  252.5 1.2 fusion.24
  253.7 21.2 %all-gather.2 = f32[1024,128]{1,0:T(8,128)S(1)} all-gather(f32[64,128]{1,0:T(8,128)S(1)} %fusion.24), channel_id=4, replica_groups=mesh['row_0'=4,'row_1'=8,'shift'=16] {'shift'}, dimensions={0}, use_global_device_ids=true | all-gather | bytes 557056 | tf_op jit(solution)/shard_map/all_gather | solution.py:47
  275.0 33.0 %all_to_all.22 = f32[32,64,128]{2,1,0:T(8,128)S(1)} all-to-all(f32[32,64,128]{2,1,0:T(8,128)S(1)} %broadcast_in_dim.75), channel_id=1, replica_groups=mesh['row_0'=4,'row_1'=8,'shift'=16] {'row_0','row_1'}, dimensions={0} | all-to-all | bytes 2097152 | tf_op jit(solution)/shard_map/all_to_all | solution.py:38
  308.0 1.0 convolution_bitcast_fusion.1
  309.1 5.8 %cholesky.44 = f32[64,64]{1,0:T(8,128)S(1)} custom-call(f32[64,64]{1,0:T(8,128)S(1)} %fusion.35), custom_call_target="Cholesky" | custom-call | tf_op jit(solution)/shard_map/jit(cholesky)/cholesky | solution.py:66
  315.0 0.6 compare_reduce_fusion.1
  315.6 0.7 fusion.30
  316.3 4.9 %custom-call.7 = f32[1,64,64]{1,2,0:T(8,128)S(1)} custom-call(f32[1,64,64]{2,1,0:T(8,128)S(1)} %fusion.30), custom_call_target="InvertDiagBlocksLowerTriangular" | custom-call | tf_op jit(solution)/shard_map/jit(_solve_triangular)/triangular_solve | solution.py:68
  321.4 1.0 fusion.17
  322.7 19.9 %all-gather.3 = f32[1024,128]{1,0:T(8,128)S(1)} all-gather(f32[64,128]{1,0:T(8,128)S(1)} %fusion.22), channel_id=5, replica_groups=mesh['row_0'=4,'row_1'=8,'shift'=16] {'shift'}, dimensions={0}, use_global_device_ids=true | all-gather | bytes 557056 | tf_op jit(solution)/shard_map/all_gather | solution.py:47
  342.7 1.1 broadcast_in_dim.76
  343.8 4.8 %all-to-all-start.3 = ((f32[32,64,128]{2,1,0:T(8,128)}), f32[32,64,128]{2,1,0:T(8,128)S(1)}, u32[]{:S(2)}, u32[]{:S(2)}) async-start(f32[32,64,128]{2,1,0:T(8,128)} %broadcast_in_dim.76), calls=%async_computation.3 | async-start | bytes 2097152 | tf_op jit(solution)/shard_map/all_to_all | solution.py:38
  348.6 25.3 %all-to-all-done.3 = f32[32,64,128]{2,1,0:T(8,128)S(1)} async-done(((f32[32,64,128]{2,1,0:T(8,128)}), f32[32,64,128]{2,1,0:T(8,128)S(1)}, u32[]{:S(2)}, u32[]{:S(2)}) %all-to-all-start.3) | async-done | bytes 1048608 | tf_op jit(solution)/shard_map/all_to_all | solution.py:38
  373.9 1.0 convolution_bitcast_fusion
  374.9 5.8 %cholesky.55 = f32[64,64]{1,0:T(8,128)S(1)} custom-call(f32[64,64]{1,0:T(8,128)S(1)} %fusion.33), custom_call_target="Cholesky" | custom-call | tf_op jit(solution)/shard_map/jit(cholesky)/cholesky | solution.py:66
  380.8 0.6 compare_reduce_fusion
  381.5 0.7 fusion.31
  382.1 4.9 %custom-call.8 = f32[1,64,64]{1,2,0:T(8,128)S(1)} custom-call(f32[1,64,64]{2,1,0:T(8,128)S(1)} %fusion.31), custom_call_target="InvertDiagBlocksLowerTriangular" | custom-call | tf_op jit(solution)/shard_map/jit(_solve_triangular)/triangular_solve | solution.py:68
  387.3 1.0 fusion.14
  388.3 0.6 constant_dynamic-slice_fusion
  (584 shorter events, 55.3 us)
Async XLA Ops:
  7.2 44.8 %copy-start.1 = (bf16[128,2,128]{2,1,0:T(2,128)(2,1)S(1)}, bf16[128,2,128]{2,1,0:T(2,128)(2,1)}, u32[]{:S(2)}) copy-start(bf16[128,2,128]{2,1,0:T(2,128)(2,1)} %param.10) | copy-start | bytes 196612
  7.2 80.5 %all-gather.6.cloned.1.call-start = ((), (), s32[]{:S(2)}) async-start(), calls=%async_computation.4 | async-start | bytes 2359296 | tf_op jit(solution)/shard_map/all_gather | solution.py:25
  42.6 44.0 %all-to-all-start.1 = ((f32[32,64,128]{2,1,0:T(8,128)}), f32[32,64,128]{2,1,0:T(8,128)S(1)}, u32[]{:S(2)}, u32[]{:S(2)}) async-start(f32[32,64,128]{2,1,0:T(8,128)} %broadcast_in_dim.74), calls=%async_computation.1 | async-start | bytes 2097152 | tf_op jit(solution)/shard_map/all_to_all | solution.py:38
  252.5 70.0 %copy-start = (f32[128,256]{1,0:T(8,128)}, f32[128,256]{1,0:T(8,128)S(1)}, u32[]{:S(2)}) copy-start(f32[128,256]{1,0:T(8,128)S(1)} %broadcast_multiply_fusion) | copy-start | bytes 393220
  343.8 30.1 %all-to-all-start.3 = ((f32[32,64,128]{2,1,0:T(8,128)}), f32[32,64,128]{2,1,0:T(8,128)S(1)}, u32[]{:S(2)}, u32[]{:S(2)}) async-start(f32[32,64,128]{2,1,0:T(8,128)} %broadcast_in_dim.76), calls=%async_computation.3 | async-start | bytes 2097152 | tf_op jit(solution)/shard_map/all_to_all | solution.py:38
Sparse Core Ops, SparseCore 0:
  19.5 65.2 all-gather.5
where the time goes:
time: 400 us; the launch traced here: 396 us
  blocking collectives  106 us (26%)
  loops' own time  99.6 us (25%)
  waiting for transfers between devices  58.6 us (15%)
  local copies, waits for them, and re-layouts  47.8 us (12%)
  other arithmetic  35.5 us (9%)
  matrix products  19.8 us (5%)
  between operations  14.3 us (4%)
  starting transfers between devices  14.1 us (4%)
    another operation x1, loops' own time, per_device(): lax.fori_loop(0, every_offset.shape[0], add_block, jnp.zeros((block_rows,...  99.6 us
    all_to_all x2, waiting for transfers between devices, sent_to_all(): return lax.all_to_all(copies, axis, split_axis=0, concat_axis=0, tiled=True)  58.6 us
    all_to_all x2, blocking collectives, sent_to_all(): return lax.all_to_all(copies, axis, split_axis=0, concat_axis=0, tiled=True)  53.7 us
    all_gather x2, blocking collectives, total_of_pieces(): tiles = lax.all_gather(x, axis)  41.1 us
    dynamic_slice x48, local copies, waits for them, and re-layouts, add_block(): offset = every_offset[which]  28.3 us
    all_to_all x2, starting transfers between devices, sent_to_all(): return lax.all_to_all(copies, axis, split_axis=0, concat_axis=0, tiled=True)  14.1 us
    dot_general x48, matrix products, add_block(): lax.dot_general(own_rows, col_rows, (((1,), (1,)), ((), ())), preferred_e...  13.9 us
    another operation x6, other arithmetic, factor(): lower_factor = jnp.linalg.cholesky(gram_matrix)  13 us
  transfers between devices with their start and end apart: 3, of which 2 were waited for; matrix products, arithmetic and copies ran while one was open for 1% of the time, Pallas kernels for 0%

commit v1 on v0

v1 whole, which is shorter than its diff:
```python
import jax
import jax.numpy as jnp
from jax import lax
from jax.experimental import pallas as pl
from jax.experimental.pallas import tpu as pltpu
from jax.sharding import Mesh
from jax.sharding import PartitionSpec as P

M = 4096
K = 64
SNAPS = 128
SHIFTS = 48
BLOCK = 128
GROUP = 4
ROW = ("row_0", "row_1")
EVERY = ("row_0", "row_1", "shift")
HALF_ROOT = 0.7071067811865476
HIGH = lax.Precision.HIGHEST


def dot_nt(a, b, precision=None):
    return lax.dot_general(
        a, b, (((1,), (1,)), ((), ())), precision=precision, preferred_element_type=jnp.float32
    )


def dot_nn(a, b, precision=None):
    return lax.dot_general(
        a, b, (((1,), (0,)), ((), ())), precision=precision, preferred_element_type=jnp.float32
    )


def sent_to_all(x, axis):
    copies = jnp.broadcast_to(x, (lax.axis_size(axis), *x.shape))
    return lax.all_to_all(copies, axis, split_axis=0, concat_axis=0, tiled=True)


def covariance_kernel(
    meta, own, after, mirror, mirror_after, tail, pieces, basis,
    cov, mapped, row_w, row_z, col_w, col_z, acc,
):
    r = meta[0]
    c = meta[1]
    flip = (
        lax.broadcasted_iota(jnp.int32, (BLOCK, BLOCK), 0)
        + lax.broadcasted_iota(jnp.int32, (BLOCK, BLOCK), 1)
        == BLOCK - 1
    ).astype(jnp.bfloat16)

    def put_window(ref, at, block, upper):
        re = block[:, :SNAPS].astype(jnp.float32) * HALF_ROOT
        im = block[:, SNAPS:].astype(jnp.float32) * HALF_ROOT
        ref[0, pl.ds(at, BLOCK), :] = jnp.where(upper, re, im)
        ref[1, pl.ds(at, BLOCK), :] = jnp.where(upper, im, -re)

    def put_mirror(ref, at, block, upper):
        turned = dot_nn(flip, block) * HALF_ROOT
        re = turned[:, :SNAPS]
        im = turned[:, SNAPS:]
        ref[0, pl.ds(at, BLOCK), :] = jnp.where(upper, re, -im)
        ref[1, pl.ds(at, BLOCK), :] = jnp.where(upper, im, re)

    row_upper = r < 16
    put_window(row_w, 0, own[...], row_upper)
    put_window(row_w, BLOCK, jnp.where(r == 31, tail[...], after[...]), row_upper)
    put_mirror(row_z, 0, jnp.where(r == 0, tail[...], mirror_after[...]), row_upper)
    put_mirror(row_z, BLOCK, mirror[...], row_upper)

    odd = [jnp.concatenate([pieces[2 * i + j, :16, :] for i in range(8)], axis=0) for j in range(2)]
    even = [jnp.concatenate([pieces[16 + 4 * i + j] for i in range(4)], axis=0) for j in range(4)]
    col_upper = c < 8
    put_window(col_w, 0, even[0], col_upper)
    put_window(col_w, BLOCK, odd[0], col_upper)
    put_window(col_w, 2 * BLOCK, jnp.where(c == 15, tail[...], even[2]), col_upper)
    put_mirror(col_z, 0, jnp.where(c == 0, tail[...], even[3]), col_upper)
    put_mirror(col_z, BLOCK, odd[1], col_upper)
    put_mirror(col_z, 2 * BLOCK, even[1], col_upper)

    acc[...] = jnp.zeros(acc.shape, jnp.float32)

    def step(at, carry):
        left, right = [], []
        for u in range(GROUP):
            o = meta[2 + at * GROUP + u]
            for plane in range(2):
                left.append(
                    (row_w[plane, pl.ds(o, BLOCK), :] + row_z[plane, pl.ds(BLOCK - o, BLOCK), :])
                    .astype(jnp.bfloat16)
                )
                right.append(
                    (col_w[plane, pl.ds(o, 2 * BLOCK), :] + col_z[plane, pl.ds(BLOCK - o, 2 * BLOCK), :])
                    .astype(jnp.bfloat16)
                )
        acc[...] += dot_nt(jnp.concatenate(left, axis=1), jnp.concatenate(right, axis=1))
        return carry

    lax.fori_loop(0, SHIFTS // GROUP, step, 0)
    block = acc[...] * (1.0 / (SNAPS * SHIFTS))
    cov[...] = block
    mapped[...] = dot_nn(basis[...], block, HIGH)


def covariance_block(meta, own, after, mirror, mirror_after, tail, pieces, basis):
    vmem = pl.BlockSpec(memory_space=pltpu.VMEM)
    return pl.pallas_call(
        covariance_kernel,
        name="covariance_block",
        in_specs=[pl.BlockSpec(memory_space=pltpu.SMEM)] + [vmem] * 7,
        out_specs=[vmem, vmem],
        out_shape=[
            jax.ShapeDtypeStruct((BLOCK, 2 * BLOCK), jnp.float32),
            jax.ShapeDtypeStruct((K, 2 * BLOCK), jnp.float32),
        ],
        scratch_shapes=[
            pltpu.VMEM((2, 2 * BLOCK, SNAPS), jnp.float32),
            pltpu.VMEM((2, 2 * BLOCK, SNAPS), jnp.float32),
            pltpu.VMEM((2, 3 * BLOCK, SNAPS), jnp.float32),
            pltpu.VMEM((2, 3 * BLOCK, SNAPS), jnp.float32),
            pltpu.VMEM((BLOCK, 2 * BLOCK), jnp.float32),
        ],
    )(meta, own, after, mirror, mirror_after, tail, pieces, basis)


def inverse_factor(gram):
    row_at = lax.broadcasted_iota(jnp.int32, (K, 2 * K), 0)
    lane_at = lax.broadcasted_iota(jnp.int32, (K, 2 * K), 1)
    eye = (lane_at == row_at + K).astype(jnp.float32)
    work = jnp.concatenate([gram, gram], axis=1)
    work = jnp.where(lane_at < K, work, eye)
    scale = jnp.zeros((K, 1), jnp.float32)
    for j in range(K):
        row = work[j : j + 1, :]
        pivot = work[j : j + 1, j : j + 1]
        factor = jnp.where(row_at[:, :1] > j, work[:, j : j + 1] / pivot, 0.0)
        scale = jnp.where(row_at[:, :1] == j, pivot, scale)
        work = work - factor * row
    return (work / jnp.sqrt(scale))[:, K:]


def image_kernel(mapped, cov, terms):
    image = mapped[...]
    terms[:, :BLOCK] = dot_nt(image, cov[...], HIGH)
    terms[:, BLOCK:] = dot_nt(image, image, HIGH)


def first_factor_kernel(total, mapped, gram):
    inverse = inverse_factor(total[:, BLOCK:])
    image = dot_nn(inverse, total[:, :BLOCK], HIGH)
    mapped[...] = image
    part = dot_nt(image, image, HIGH)
    gram[...] = jnp.concatenate([part[: K // 2], part[K // 2 :]], axis=1)


def last_factor_kernel(grams, mapped, basis):
    total = jnp.sum(grams[...], axis=0)
    gram = jnp.concatenate([total[:, :K], total[:, K:]], axis=0)
    basis[...] = dot_nn(inverse_factor(gram), mapped[...], HIGH)


def local_call(kernel, name, shapes, *operands):
    return pl.pallas_call(
        kernel,
        name=name,
        out_shape=[jax.ShapeDtypeStruct(s, jnp.float32) for s in shapes],
    )(*operands)


def total_over(terms, axis):
    n = lax.axis_size(axis)
    tiles = terms.reshape(n, terms.shape[0] // n, terms.shape[1])
    tiles = lax.all_to_all(tiles, axis, split_axis=0, concat_axis=0, tiled=True)
    return sent_to_all(tiles.sum(axis=0), axis).reshape(terms.shape)


def piece_routes():
    routes = []
    for b in range(32):
        for q in range(16):
            if b % 2:
                c = (b - 1) // 2 if q % 2 == 0 else (31 - b) // 2
                to = q
            else:
                c = (b // 2, (30 - b) // 2, (b // 2 - 1) % 16, (16 - b // 2) % 16)[q % 4]
                to = q + 16
            routes.append((b * 16 + q, to * 16 + c))
    return routes


def per_device(snapshots, tail_sensors, shift_offsets, start_basis):
    r = lax.axis_index(ROW)
    c = lax.axis_index("shift")
    own = snapshots.reshape(BLOCK, 2 * SNAPS)
    tail = tail_sensors.reshape(BLOCK, 2 * SNAPS)
    offsets = jnp.zeros((16, 2 * SNAPS), jnp.bfloat16)
    offsets = lax.dynamic_update_slice(offsets, shift_offsets.astype(jnp.bfloat16)[None], (0, 0))
    odd_piece = jnp.concatenate([lax.dynamic_slice_in_dim(own, 16 * (c // 2), 16, 0), offsets], 0)
    even_piece = lax.dynamic_slice_in_dim(own, 32 * (c // 4), 32, 0)
    piece = jnp.where(r % 2 == 1, odd_piece, even_piece)
    piece = lax.ppermute(piece, EVERY, piece_routes())
    after = lax.ppermute(own, ROW, [(i, (i - 1) % 32) for i in range(32)])
    mirror = lax.ppermute(own, ROW, [(i, 31 - i) for i in range(32)])
    mirror_after = lax.ppermute(own, ROW, [(i, (32 - i) % 32) for i in range(32)])
    pieces = sent_to_all(piece, ROW)
    every_offset = pieces[:16, 16, :3].astype(jnp.int32).reshape(-1)
    meta = jnp.concatenate([jnp.stack([r, c]).astype(jnp.int32), every_offset])
    cov, mapped = covariance_block(
        meta, own, after, mirror, mirror_after, tail, pieces, start_basis
    )
    mapped = total_over(mapped, ROW)
    (terms,) = local_call(image_kernel, "image", [(K, BLOCK + K)], mapped, cov)
    total = total_over(terms, "shift")
    mapped, gram = local_call(
        first_factor_kernel, "first_factor", [(K, BLOCK), (K // 2, 2 * K)], total
    )
    grams = sent_to_all(gram, ROW)
    (basis,) = local_call(last_factor_kernel, "last_factor", [(K, BLOCK)], grams, mapped)
    return (cov, basis)


def solution(mesh):
    split = Mesh(mesh.devices.reshape(4, 8, mesh.shape["shift"]), ("row_0", "row_1", "shift"))
    in_specs = (P(ROW, None, None), P(), P("shift"), P(None, ROW))
    out_specs = (P(ROW, "shift"), P(None, ROW))
    return jax.shard_map(
        per_device, mesh=split, in_specs=in_specs, out_specs=out_specs, check_vma=False
    )
```

time: 400 us -> 160 us (0.40)
  the two profiles are of different devices: /device:TPU:1 before, /device:TPU:8 now
where the time goes in v1:
time: 160 us; the launch traced here: 159 us
  blocking collectives  80.5 us (50%)
  starting transfers between devices  39.1 us (24%)
  Pallas kernels  24.4 us (15%)
  local copies, waits for them, and re-layouts  7.48 us (5%)
  waiting for transfers between devices  5.58 us (3%)
    all_to_all x3, blocking collectives, sent_to_all(): return lax.all_to_all(copies, axis, split_axis=0, concat_axis=0, tiled=True)  46.6 us
    all_to_all x2, blocking collectives, total_over(): tiles = lax.all_to_all(tiles, axis, split_axis=0, concat_axis=0, tiled=True)  33.9 us
    pallas_call x3, Pallas kernels, local_call(): pl.pallas_call(kernel, name=name, out_shape=[jax.ShapeDtypeStruct(s, jnp....  17.4 us
    all_to_all x1, starting transfers between devices, sent_to_all(): return lax.all_to_all(copies, axis, split_axis=0, concat_axis=0, tiled=True)  15.4 us
    ppermute x1, starting transfers between devices, per_device(): mirror = lax.ppermute(own, ROW, [(i, 31 - i) for i in range(32)])  8.9 us
    ppermute x1, starting transfers between devices, per_device(): piece = lax.ppermute(piece, EVERY, piece_routes())  7.7 us
    pallas_call x1, Pallas kernels, covariance_block(): pl.pallas_call(covariance_kernel, name='covariance_block', in_specs=[pl.B...  7.05 us
    ppermute x1, starting transfers between devices, per_device(): lax.ppermute(own, ROW, [(i, (32 - i) % 32) for i in range(32)])  4.91 us
  transfers between devices with their start and end apart: 5, of which 3 were waited for; matrix products, arithmetic and copies ran while one was open for 1% of the time, Pallas kernels for 0%

profile of v1, /device:TPU:8, one launch (start us, length us, event | category | flops | bytes accessed | tf_op | source)
XLA Modules:
  0.0 158.6 jit_solution(9451190666976910880)
XLA Ops:
  0.6 0.0 copy-start.5
  0.7 0.8 copy-done.5
  1.5 0.0 copy-start.7
  1.5 0.6 copy-done.7
  2.1 0.0 copy-start.1
  2.2 7.7 %collective-permute-start = (bf16[32,256]{1,0:T(8,128)(2,1)S(1)}, bf16[32,256]{1,0:T(8,128)(2,1)S(1)}, u32[]{:S(2)}, u32[]{:S(2)}) collective-permute-start(bf16[32,256]{1,0:T(8,128)(2,1)S(1)} %fusion.2), channel_id=1, source_target_pairs={{0,256},{1,287},{2,303},{3,304},{4,320},{5,351},{6,367},{7,368},{8... | collective-permute-start | bytes 49160 | tf_op jit(solution)/shard_map/ppermute | solution.py:199
  9.9 1.6 collective-permute-done
  11.4 0.8 broadcast_in_dim.17
  12.3 0.0 copy-start.6
  12.3 15.4 %all-to-all-start = ((bf16[32,32,256]{2,1,0:T(8,128)(2,1)}), bf16[32,32,256]{2,1,0:T(8,128)(2,1)S(1)}, u32[]{:S(2)}, u32[]{:S(2)}) async-start(bf16[32,32,256]{2,1,0:T(8,128)(2,1)} %broadcast_in_dim.17), calls=%async_computation | async-start | bytes 1048576 | tf_op jit(solution)/shard_map/all_to_all | solution.py:35
  27.7 2.1 %collective-permute-start.1 = (bf16[128,256]{1,0:T(8,128)(2,1)S(1)}, bf16[128,256]{1,0:T(8,128)(2,1)S(1)}, u32[]{:S(2)}, u32[]{:S(2)}) collective-permute-start(bf16[128,256]{1,0:T(8,128)(2,1)S(1)} %bitcast.14), channel_id=1, source_target_pairs={{0,496},{16,0},{32,16},{48,32},{64,48},{80,64},{96,80},{112,96},{1... | collective-permute-start | bytes 196616 | tf_op jit(solution)/shard_map/ppermute | solution.py:200
  29.9 8.9 %collective-permute-start.2 = (bf16[128,256]{1,0:T(8,128)(2,1)S(1)}, bf16[128,256]{1,0:T(8,128)(2,1)S(1)}, u32[]{:S(2)}, u32[]{:S(2)}) collective-permute-start(bf16[128,256]{1,0:T(8,128)(2,1)S(1)} %bitcast.15), channel_id=1, source_target_pairs={{0,496},{16,480},{32,464},{48,448},{64,432},{80,416},{96,400},{112... | collective-permute-start | bytes 196616 | tf_op jit(solution)/shard_map/ppermute | solution.py:201
  38.8 0.0 copy-done.1
  38.8 4.9 %collective-permute-start.3 = (bf16[128,256]{1,0:T(8,128)(2,1)S(1)}, bf16[128,256]{1,0:T(8,128)(2,1)S(1)}, u32[]{:S(2)}, u32[]{:S(2)}) collective-permute-start(bf16[128,256]{1,0:T(8,128)(2,1)S(1)} %bitcast.16), channel_id=1, source_target_pairs={{0,0},{16,496},{32,480},{48,464},{64,448},{80,432},{96,416},{112,4... | collective-permute-start | bytes 196616 | tf_op jit(solution)/shard_map/ppermute | solution.py:202
  43.7 0.0 copy-done.6
  43.7 0.6 copy.10
  44.3 1.9 %all-to-all-done.pieces = bf16[32,32,256]{2,1,0:T(8,128)(2,1)S(1)} async-done(((bf16[32,32,256]{2,1,0:T(8,128)(2,1)}), bf16[32,32,256]{2,1,0:T(8,128)(2,1)S(1)}, u32[]{:S(2)}, u32[]{:S(2)}) %all-to-all-start) | async-done | bytes 524320 | tf_op jit(solution)/shard_map/all_to_all | solution.py:35
  46.2 0.0 copy-start
  46.3 0.1 reshape.32
  46.3 0.7 pad_add_fusion.meta
  47.0 0.0 collective-permute-done.1.after
  47.0 0.0 copy-start.2
  47.0 0.0 collective-permute-done.2.mirror
  47.0 0.0 copy-start.3
  47.0 2.1 %collective-permute-done.3.mirror_after = bf16[128,256]{1,0:T(8,128)(2,1)S(1)} collective-permute-done((bf16[128,256]{1,0:T(8,128)(2,1)S(1)}, bf16[128,256]{1,0:T(8,128)(2,1)S(1)}, u32[]{:S(2)}, u32[]{:S(2)}) %collective-permute-start.3) | collective-permute-done | bytes 65568 | tf_op jit(solution)/shard_map/ppermute | solution.py:202
  49.1 0.0 copy-start.4
  49.1 0.0 copy-done
  49.2 0.0 copy-done.2
  49.2 0.0 copy-done.3
  49.2 0.6 copy-done.4
  49.8 7.0 %covariance_block.1 = (f32[128,256]{1,0:T(8,128)}, f32[64,256]{1,0:T(8,128)}) custom-call(s32[50]{0:T(128)} %pad_add_fusion.meta, bf16[128,256]{1,0:T(8,128)(2,1)} %bitcast.17, bf16[128,256]{1,0:T(8,128)(2,1)} %copy-done.2, bf16[128,256]{1,0:T(8,128)(2,1)} %copy-done.3, bf16[128,256]{1,0:T(8,128)(2,1)} %copy-done.4, bf16[128,256]{1,0:T(8,128)(2,1)} %bitcast.18, ...), custom_call_target="tpu_custom_call" | custom-call | tf_op jit(solution)/shard_map/covariance_block/pallas_call | solution.py:105
  56.8 0.9 reshape.28
  57.7 15.0 %all_to_all.30 = f32[32,2,256]{2,1,0:T(2,128)S(1)} all-to-all(f32[32,2,256]{2,1,0:T(2,128)S(1)} %reshape.28), channel_id=1, replica_groups=mesh['row_0'=4,'row_1'=8,'shift'=16] {'row_0','row_1'}, dimensions={0} | all-to-all | bytes 131072 | tf_op jit(solution)/shard_map/all_to_all | solution.py:171
  72.8 13.2 %all_to_all.31 = f32[32,2,256]{2,1,0:T(2,128)S(1)} all-to-all(f32[32,2,256]{2,1,0:T(2,128)S(1)} %broadcast_in_dim.18), channel_id=1, replica_groups=mesh['row_0'=4,'row_1'=8,'shift'=16] {'row_0','row_1'}, dimensions={0} | all-to-all | bytes 131072 | tf_op jit(solution)/shard_map/all_to_all | solution.py:35
  86.0 0.7 reshape.29.mapped
  86.6 1.9 %image.1 = f32[64,192]{1,0:T(8,128)} custom-call(f32[64,256]{1,0:T(8,128)} %reshape.29.mapped, f32[128,256]{1,0:T(8,128)} %get-tuple-element.4.cov), custom_call_target="tpu_custom_call" | custom-call | tf_op jit(solution)/shard_map/image/pallas_call | solution.py:161
  88.5 0.9 reshape.30
  89.4 18.9 %all_to_all.32 = f32[16,4,192]{2,1,0:T(4,128)S(1)} all-to-all(f32[16,4,192]{2,1,0:T(4,128)S(1)} %reshape.30), channel_id=1, replica_groups=mesh['row_0'=4,'row_1'=8,'shift'=16] {'shift'}, dimensions={0} | all-to-all | bytes 98304 | tf_op jit(solution)/shard_map/all_to_all | solution.py:171
  108.3 10.4 %all_to_all.33 = f32[16,4,192]{2,1,0:T(4,128)S(1)} all-to-all(f32[16,4,192]{2,1,0:T(4,128)S(1)} %broadcast_in_dim.19), channel_id=1, replica_groups=mesh['row_0'=4,'row_1'=8,'shift'=16] {'shift'}, dimensions={0} | all-to-all | bytes 98304 | tf_op jit(solution)/shard_map/all_to_all | solution.py:35
  118.7 0.6 reshape.31.total
  119.3 7.9 %first_factor.1 = (f32[64,128]{1,0:T(8,128)}, f32[32,128]{1,0:T(8,128)}) custom-call(f32[64,192]{1,0:T(8,128)} %reshape.31.total), custom_call_target="tpu_custom_call" | custom-call | tf_op jit(solution)/shard_map/first_factor/pallas_call | solution.py:161
  127.2 0.8 broadcast_in_dim.20
  127.9 23.1 %all_to_all.34.grams = f32[32,32,128]{2,1,0:T(8,128)} all-to-all(f32[32,32,128]{2,1,0:T(8,128)S(1)} %broadcast_in_dim.20), channel_id=1, replica_groups=mesh['row_0'=4,'row_1'=8,'shift'=16] {'row_0','row_1'}, dimensions={0} | all-to-all | bytes 1048576 | tf_op jit(solution)/shard_map/all_to_all | solution.py:35
  151.0 7.6 %last_factor.1 = f32[64,128]{1,0:T(8,128)} custom-call(f32[32,32,128]{2,1,0:T(8,128)} %all_to_all.34.grams, f32[64,128]{1,0:T(8,128)} %get-tuple-element.9.mapped), custom_call_target="tpu_custom_call" | custom-call | tf_op jit(solution)/shard_map/last_factor/pallas_call | solution.py:161
  (9 shorter events, 0.2 us)
Async XLA Ops:
  0.6 0.8 copy-start.5
  1.5 0.7 copy-start.7
  2.1 36.6 %copy-start.1 = (bf16[16,8,2,128]{3,1,2,0:T(8,128)(2,1)}, bf16[16,8,2,128]{3,1,2,0:T(8,128)(2,1)S(1)}, u32[]{:S(2)}) copy-start(bf16[16,8,2,128]{3,1,2,0:T(8,128)(2,1)S(1)} %copy.11) | copy-start | bytes 196612
  2.2 9.3 %collective-permute-start = (bf16[32,256]{1,0:T(8,128)(2,1)S(1)}, bf16[32,256]{1,0:T(8,128)(2,1)S(1)}, u32[]{:S(2)}, u32[]{:S(2)}) collective-permute-start(bf16[32,256]{1,0:T(8,128)(2,1)S(1)} %fusion.2), channel_id=1, source_target_pairs={{0,256},{1,287},{2,303},{3,304},{4,320},{5,351},{6,367},{7,368},{8... | collective-permute-start | bytes 49160 | tf_op jit(solution)/shard_map/ppermute | solution.py:199
  12.3 31.4 %copy-start.6 = (bf16[128,2,128]{2,1,0:T(2,128)(2,1)S(1)}, bf16[128,2,128]{2,1,0:T(2,128)(2,1)}, u32[]{:S(2)}) copy-start(bf16[128,2,128]{2,1,0:T(2,128)(2,1)} %param.5) | copy-start | bytes 196612
  12.3 33.9 %all-to-all-start = ((bf16[32,32,256]{2,1,0:T(8,128)(2,1)}), bf16[32,32,256]{2,1,0:T(8,128)(2,1)S(1)}, u32[]{:S(2)}, u32[]{:S(2)}) async-start(bf16[32,32,256]{2,1,0:T(8,128)(2,1)} %broadcast_in_dim.17), calls=%async_computation | async-start | bytes 1048576 | tf_op jit(solution)/shard_map/all_to_all | solution.py:35
  27.7 19.3 %collective-permute-start.1 = (bf16[128,256]{1,0:T(8,128)(2,1)S(1)}, bf16[128,256]{1,0:T(8,128)(2,1)S(1)}, u32[]{:S(2)}, u32[]{:S(2)}) collective-permute-start(bf16[128,256]{1,0:T(8,128)(2,1)S(1)} %bitcast.14), channel_id=1, source_target_pairs={{0,496},{16,0},{32,16},{48,32},{64,48},{80,64},{96,80},{112,96},{1... | collective-permute-start | bytes 196616 | tf_op jit(solution)/shard_map/ppermute | solution.py:200
  29.9 17.2 %collective-permute-start.2 = (bf16[128,256]{1,0:T(8,128)(2,1)S(1)}, bf16[128,256]{1,0:T(8,128)(2,1)S(1)}, u32[]{:S(2)}, u32[]{:S(2)}) collective-permute-start(bf16[128,256]{1,0:T(8,128)(2,1)S(1)} %bitcast.15), channel_id=1, source_target_pairs={{0,496},{16,480},{32,464},{48,448},{64,432},{80,416},{96,400},{112... | collective-permute-start | bytes 196616 | tf_op jit(solution)/shard_map/ppermute | solution.py:201
  38.8 10.4 %collective-permute-start.3 = (bf16[128,256]{1,0:T(8,128)(2,1)S(1)}, bf16[128,256]{1,0:T(8,128)(2,1)S(1)}, u32[]{:S(2)}, u32[]{:S(2)}) collective-permute-start(bf16[128,256]{1,0:T(8,128)(2,1)S(1)} %bitcast.16), channel_id=1, source_target_pairs={{0,0},{16,496},{32,480},{48,464},{64,448},{80,432},{96,416},{112,4... | collective-permute-start | bytes 196616 | tf_op jit(solution)/shard_map/ppermute | solution.py:202
  46.2 2.9 %copy-start = (bf16[32,32,256]{2,1,0:T(8,128)(2,1)}, bf16[32,32,256]{2,1,0:T(8,128)(2,1)S(1)}, u32[]{:S(2)}) copy-start(bf16[32,32,256]{2,1,0:T(8,128)(2,1)S(1)} %all-to-all-done.pieces) | copy-start | bytes 1572868
  47.0 2.1 %copy-start.2 = (bf16[128,256]{1,0:T(8,128)(2,1)}, bf16[128,256]{1,0:T(8,128)(2,1)S(1)}, u32[]{:S(2)}) copy-start(bf16[128,256]{1,0:T(8,128)(2,1)S(1)} %collective-permute-done.1.after) | copy-start | bytes 196612
  47.0 2.1 %copy-start.3 = (bf16[128,256]{1,0:T(8,128)(2,1)}, bf16[128,256]{1,0:T(8,128)(2,1)S(1)}, u32[]{:S(2)}) copy-start(bf16[128,256]{1,0:T(8,128)(2,1)S(1)} %collective-permute-done.2.mirror) | copy-start | bytes 196612
  49.1 0.6 copy-start.4

commit v2 on v1

--- a/solution.py
+++ b/solution.py
@@ -11,7 +11,7 @@
 SNAPS = 128
 SHIFTS = 48
 BLOCK = 128
-GROUP = 4
+GROUP = 2
 ROW = ("row_0", "row_1")
 EVERY = ("row_0", "row_1", "shift")
 HALF_ROOT = 0.7071067811865476
@@ -36,11 +36,11 @@
 
 
 def covariance_kernel(
-    meta, own, after, mirror, mirror_after, tail, pieces, basis,
+    place, offsets, own, after, mirror, mirror_after, tail, pieces, basis,
     cov, mapped, row_w, row_z, col_w, col_z, acc,
 ):
-    r = meta[0]
-    c = meta[1]
+    r = place[0]
+    c = place[1]
     flip = (
         lax.broadcasted_iota(jnp.int32, (BLOCK, BLOCK), 0)
         + lax.broadcasted_iota(jnp.int32, (BLOCK, BLOCK), 1)
@@ -80,8 +80,8 @@
 
     def step(at, carry):
         left, right = [], []
-        for u in range(GROUP):
-            o = meta[2 + at * GROUP + u]
+        for u in range(3 * GROUP):
+            o = offsets[at * GROUP + u // 3, u % 3]
             for plane in range(2):
                 left.append(
                     (row_w[plane, pl.ds(o, BLOCK), :] + row_z[plane, pl.ds(BLOCK - o, BLOCK), :])
@@ -94,22 +94,24 @@
         acc[...] += dot_nt(jnp.concatenate(left, axis=1), jnp.concatenate(right, axis=1))
         return carry
 
-    lax.fori_loop(0, SHIFTS // GROUP, step, 0)
+    lax.fori_loop(0, 16 // GROUP, step, 0)
     block = acc[...] * (1.0 / (SNAPS * SHIFTS))
     cov[...] = block
-    mapped[...] = dot_nn(basis[...], block, HIGH)
-
-
-def covariance_block(meta, own, after, mirror, mirror_after, tail, pieces, basis):
+    image = dot_nn(basis[...], block, HIGH)
+    for p in range(32):
+        mapped[p] = image[4 * (p // 2) : 4 * (p // 2) + 4, SNAPS * (p % 2) : SNAPS * (p % 2) + SNAPS]
+
+
+def covariance_block(place, offsets, own, after, mirror, mirror_after, tail, pieces, basis):
     vmem = pl.BlockSpec(memory_space=pltpu.VMEM)
     return pl.pallas_call(
         covariance_kernel,
         name="covariance_block",
-        in_specs=[pl.BlockSpec(memory_space=pltpu.SMEM)] + [vmem] * 7,
+        in_specs=[pl.BlockSpec(memory_space=pltpu.SMEM)] * 2 + [vmem] * 7,
         out_specs=[vmem, vmem],
         out_shape=[
             jax.ShapeDtypeStruct((BLOCK, 2 * BLOCK), jnp.float32),
-            jax.ShapeDtypeStruct((K, 2 * BLOCK), jnp.float32),
+            jax.ShapeDtypeStruct((32, 4, SNAPS), jnp.float32),
         ],
         scratch_shapes=[
             pltpu.VMEM((2, 2 * BLOCK, SNAPS), jnp.float32),
@@ -118,37 +120,52 @@
             pltpu.VMEM((2, 3 * BLOCK, SNAPS), jnp.float32),
             pltpu.VMEM((BLOCK, 2 * BLOCK), jnp.float32),
         ],
-    )(meta, own, after, mirror, mirror_after, tail, pieces, basis)
+    )(place, offsets, own, after, mirror, mirror_after, tail, pieces, basis)
 
 
 def inverse_factor(gram):
-    row_at = lax.broadcasted_iota(jnp.int32, (K, 2 * K), 0)
-    lane_at = lax.broadcasted_iota(jnp.int32, (K, 2 * K), 1)
-    eye = (lane_at == row_at + K).astype(jnp.float32)
-    work = jnp.concatenate([gram, gram], axis=1)
-    work = jnp.where(lane_at < K, work, eye)
-    scale = jnp.zeros((K, 1), jnp.float32)
+    row_at = lax.broadcasted_iota(jnp.int32, (8, 2 * K), 0)
+    lane_at = lax.broadcasted_iota(jnp.int32, (8, 2 * K), 1)
+    tiles, done = [], []
+    for t in range(K // 8):
+        part = gram[8 * t : 8 * t + 8]
+        eye = (lane_at == row_at + (K + 8 * t)).astype(jnp.float32)
+        tiles.append(jnp.where(lane_at < K, jnp.concatenate([part, part], axis=1), eye))
+        done.append(jnp.zeros((8, 2 * K), jnp.float32))
     for j in range(K):
-        row = work[j : j + 1, :]
-        pivot = work[j : j + 1, j : j + 1]
-        factor = jnp.where(row_at[:, :1] > j, work[:, j : j + 1] / pivot, 0.0)
-        scale = jnp.where(row_at[:, :1] == j, pivot, scale)
-        work = work - factor * row
-    return (work / jnp.sqrt(scale))[:, K:]
+        at, s = divmod(j, 8)
+        row = tiles[at][s : s + 1, :]
+        cols = [jnp.broadcast_to(tiles[t][:, j : j + 1], (8, 2 * K)) for t in range(at, K // 8)]
+        pivot = cols[0][s : s + 1, :]
+        scaled = row * (1.0 / pivot)
+        done[at] = jnp.where(row_at == s, row / jnp.sqrt(pivot), done[at])
+        tiles[at] = jnp.where(row_at > s, tiles[at] - cols[0] * scaled, tiles[at])
+        for t in range(at + 1, K // 8):
+            tiles[t] = tiles[t] - cols[t - at] * scaled
+    return jnp.concatenate(done, axis=0)[:, K:]
 
 
 def image_kernel(mapped, cov, terms):
-    image = mapped[...]
-    terms[:, :BLOCK] = dot_nt(image, cov[...], HIGH)
-    terms[:, BLOCK:] = dot_nt(image, image, HIGH)
-
-
-def first_factor_kernel(total, mapped, gram):
-    inverse = inverse_factor(total[:, BLOCK:])
-    image = dot_nn(inverse, total[:, :BLOCK], HIGH)
+    image = jnp.concatenate(
+        [jnp.concatenate([mapped[2 * i], mapped[2 * i + 1]], axis=1) for i in range(16)], axis=0
+    )
+    product = dot_nt(image, cov[...], HIGH)
+    gram = dot_nt(image, image, HIGH)
+    gram = jnp.concatenate([gram, gram], axis=1)
+    for t in range(8):
+        terms[2 * t] = product[8 * t : 8 * t + 8]
+        terms[2 * t + 1] = gram[8 * t : 8 * t + 8]
+
+
+def first_factor_kernel(total, mapped, grams):
+    product = jnp.concatenate([total[2 * t] for t in range(8)], axis=0)
+    gram = jnp.concatenate([total[2 * t + 1] for t in range(8)], axis=0)
+    image = dot_nn(inverse_factor(gram[:, :K]), product, HIGH)
     mapped[...] = image
     part = dot_nt(image, image, HIGH)
-    gram[...] = jnp.concatenate([part[: K // 2], part[K // 2 :]], axis=1)
+    part = jnp.concatenate([part[: K // 2], part[K // 2 :]], axis=1)
+    for i in range(grams.shape[0]):
+        grams[i] = part
 
 
 def last_factor_kernel(grams, mapped, basis):
@@ -165,11 +182,12 @@
     )(*operands)
 
 
-def total_over(terms, axis):
-    n = lax.axis_size(axis)
-    tiles = terms.reshape(n, terms.shape[0] // n, terms.shape[1])
-    tiles = lax.all_to_all(tiles, axis, split_axis=0, concat_axis=0, tiled=True)
-    return sent_to_all(tiles.sum(axis=0), axis).reshape(terms.shape)
+def exchanged(tiles, axis):
+    return lax.all_to_all(tiles, axis, split_axis=0, concat_axis=0, tiled=True)
+
+
+def total_over(tiles, axis):
+    return sent_to_all(exchanged(tiles, axis).sum(axis=0), axis)
 
 
 def piece_routes():
@@ -201,18 +219,18 @@
     mirror = lax.ppermute(own, ROW, [(i, 31 - i) for i in range(32)])
     mirror_after = lax.ppermute(own, ROW, [(i, (32 - i) % 32) for i in range(32)])
     pieces = sent_to_all(piece, ROW)
-    every_offset = pieces[:16, 16, :3].astype(jnp.int32).reshape(-1)
-    meta = jnp.concatenate([jnp.stack([r, c]).astype(jnp.int32), every_offset])
+    every_offset = pieces[:16, 16, :3].astype(jnp.int32)
+    place = jnp.stack([r, c]).astype(jnp.int32)
     cov, mapped = covariance_block(
-        meta, own, after, mirror, mirror_after, tail, pieces, start_basis
+        place, every_offset, own, after, mirror, mirror_after, tail, pieces, start_basis
     )
     mapped = total_over(mapped, ROW)
-    (terms,) = local_call(image_kernel, "image", [(K, BLOCK + K)], mapped, cov)
+    (terms,) = local_call(image_kernel, "image", [(16, 8, SNAPS)], mapped, cov)
     total = total_over(terms, "shift")
-    mapped, gram = local_call(
-        first_factor_kernel, "first_factor", [(K, BLOCK), (K // 2, 2 * K)], total
-    )
-    grams = sent_to_all(gram, ROW)
+    mapped, grams = local_call(
+        first_factor_kernel, "first_factor", [(K, BLOCK), (4, K // 2, 2 * K)], total
+    )
+    grams = sent_to_all(exchanged(grams, "row_0").sum(axis=0), "row_1")
     (basis,) = local_call(last_factor_kernel, "last_factor", [(K, BLOCK)], grams, mapped)
     return (cov, basis)
 

time: 160 us -> 153 us (0.956)
  the two profiles are of different devices: /device:TPU:8 before, /device:TPU:1 now
where the time goes in v2:
time: 153 us; the launch traced here: 152 us
  blocking collectives  86 us (56%)
  starting transfers between devices  32.5 us (21%)
  Pallas kernels  23 us (15%)
  waiting for transfers between devices  5.39 us (4%)
  local copies, waits for them, and re-layouts  2.95 us (2%)
    all_to_all x3, blocking collectives, exchanged(): return lax.all_to_all(tiles, axis, split_axis=0, concat_axis=0, tiled=True)  51.4 us
    all_to_all x3, blocking collectives, sent_to_all(): return lax.all_to_all(copies, axis, split_axis=0, concat_axis=0, tiled=True)  34.6 us
    pallas_call x3, Pallas kernels, local_call(): pl.pallas_call(kernel, name=name, out_shape=[jax.ShapeDtypeStruct(s, jnp....  16.5 us
    ppermute x1, starting transfers between devices, per_device(): piece = lax.ppermute(piece, EVERY, piece_routes())  15 us
    all_to_all x1, starting transfers between devices, sent_to_all(): return lax.all_to_all(copies, axis, split_axis=0, concat_axis=0, tiled=True)  7.28 us
    pallas_call x1, Pallas kernels, covariance_block(): pl.pallas_call(covariance_kernel, name='covariance_block', in_specs=[pl.B...  6.57 us
    ppermute x1, starting transfers between devices, per_device(): after = lax.ppermute(own, ROW, [(i, (i - 1) % 32) for i in range(32)])  6.55 us
    ppermute x1, waiting for transfers between devices, per_device(): mirror = lax.ppermute(own, ROW, [(i, 31 - i) for i in range(32)])  3.67 us
  transfers between devices with their start and end apart: 5, of which 3 were waited for; matrix products, arithmetic and copies ran while one was open for 1% of the time, Pallas kernels for 0%

profile of v2, /device:TPU:1, one launch (start us, length us, event | category | flops | bytes accessed | tf_op | source)
XLA Modules:
  0.0 152.2 jit_solution(13994028030066563147)
XLA Ops:
  0.6 0.0 copy-start.5
  0.7 0.0 copy-start.7
  0.7 0.6 copy-done.7
  1.3 0.1 copy-done.5
  1.5 0.0 copy-start.1
  1.6 15.0 %collective-permute-start = (bf16[32,256]{1,0:T(8,128)(2,1)S(1)}, bf16[32,256]{1,0:T(8,128)(2,1)S(1)}, u32[]{:S(2)}, u32[]{:S(2)}) collective-permute-start(bf16[32,256]{1,0:T(8,128)(2,1)S(1)} %fusion.2), channel_id=1, source_target_pairs={{0,256},{1,287},{2,303},{3,304},{4,320},{5,351},{6,367},{7,368},{8... | collective-permute-start | bytes 49160 | tf_op jit(solution)/shard_map/ppermute | solution.py:217
  16.5 0.8 collective-permute-done
  17.4 0.8 broadcast_in_dim.17
  18.2 0.0 copy-start.6
  18.2 7.3 %all-to-all-start = ((bf16[32,32,256]{2,1,0:T(8,128)(2,1)}), bf16[32,32,256]{2,1,0:T(8,128)(2,1)S(1)}, u32[]{:S(2)}, u32[]{:S(2)}) async-start(bf16[32,32,256]{2,1,0:T(8,128)(2,1)} %broadcast_in_dim.17), calls=%async_computation | async-start | bytes 1048576 | tf_op jit(solution)/shard_map/all_to_all | solution.py:35
  25.5 6.6 %collective-permute-start.1 = (bf16[128,256]{1,0:T(8,128)(2,1)S(1)}, bf16[128,256]{1,0:T(8,128)(2,1)S(1)}, u32[]{:S(2)}, u32[]{:S(2)}) collective-permute-start(bf16[128,256]{1,0:T(8,128)(2,1)S(1)} %bitcast.15), channel_id=1, source_target_pairs={{0,496},{16,0},{32,16},{48,32},{64,48},{80,64},{96,80},{112,96},{1... | collective-permute-start | bytes 196616 | tf_op jit(solution)/shard_map/ppermute | solution.py:218
  32.1 3.1 %collective-permute-start.2 = (bf16[128,256]{1,0:T(8,128)(2,1)S(1)}, bf16[128,256]{1,0:T(8,128)(2,1)S(1)}, u32[]{:S(2)}, u32[]{:S(2)}) collective-permute-start(bf16[128,256]{1,0:T(8,128)(2,1)S(1)} %bitcast.16), channel_id=1, source_target_pairs={{0,496},{16,480},{32,464},{48,448},{64,432},{80,416},{96,400},{112... | collective-permute-start | bytes 196616 | tf_op jit(solution)/shard_map/ppermute | solution.py:219
  35.2 0.0 copy-done.1
  35.2 0.7 collective-permute-start.3
  35.8 0.0 copy-done.6
  35.8 0.6 copy.15
  36.5 0.7 pad_add_fusion.place
  37.1 0.9 all-to-all-done.pieces
  38.0 0.0 copy-start
  38.0 0.7 slice_convert_fusion
  38.7 0.0 collective-permute-done.1.after
  38.7 0.0 copy-start.2
  38.7 3.7 %collective-permute-done.2.mirror = bf16[128,256]{1,0:T(8,128)(2,1)S(1)} collective-permute-done((bf16[128,256]{1,0:T(8,128)(2,1)S(1)}, bf16[128,256]{1,0:T(8,128)(2,1)S(1)}, u32[]{:S(2)}, u32[]{:S(2)}) %collective-permute-start.2) | collective-permute-done | bytes 65568 | tf_op jit(solution)/shard_map/ppermute | solution.py:219
  42.3 0.0 copy-start.3
  42.3 0.0 collective-permute-done.3.mirror_after
  42.3 0.0 copy-start.4
  42.3 0.0 copy-done
  42.4 0.0 copy-done.2
  42.4 0.6 copy-done.3
  43.0 0.0 copy-done.4
  43.0 6.6 %covariance_block.1 = (f32[128,256]{1,0:T(8,128)}, f32[32,4,128]{2,1,0:T(4,128)}) custom-call(s32[2]{0:T(128)} %pad_add_fusion.place, s32[16,3]{1,0:T(8,128)} %bitcast.22, bf16[128,256]{1,0:T(8,128)(2,1)} %bitcast.18, bf16[128,256]{1,0:T(8,128)(2,1)} %copy-done.2, bf16[128,256]{1,0:T(8,128)(2,1)} %copy-done.3, bf16[128,256]{1,0:T(8,128)(2,1)} %copy-done.4, ...), custom_call_target="tpu_custom_call" | custom-call | tf_op jit(solution)/shard_map/covariance_block/pallas_call | solution.py:107
  49.5 18.3 %all_to_all.35 = f32[32,4,128]{2,1,0:T(4,128)S(1)} all-to-all(f32[32,4,128]{2,1,0:T(4,128)} %get-tuple-element.7), channel_id=1, replica_groups=mesh['row_0'=4,'row_1'=8,'shift'=16] {'row_0','row_1'}, dimensions={0} | all-to-all | bytes 131072 | tf_op jit(solution)/shard_map/all_to_all | solution.py:186
  67.9 12.5 %all_to_all.36.mapped = f32[32,4,128]{2,1,0:T(4,128)} all-to-all(f32[32,4,128]{2,1,0:T(4,128)S(1)} %broadcast_in_dim.18), channel_id=1, replica_groups=mesh['row_0'=4,'row_1'=8,'shift'=16] {'row_0','row_1'}, dimensions={0} | all-to-all | bytes 131072 | tf_op jit(solution)/shard_map/all_to_all | solution.py:35
  80.4 1.9 %image.1 = f32[16,8,128]{2,1,0:T(8,128)} custom-call(f32[32,4,128]{2,1,0:T(4,128)} %all_to_all.36.mapped, f32[128,256]{1,0:T(8,128)} %get-tuple-element.4.cov), custom_call_target="tpu_custom_call" | custom-call | tf_op jit(solution)/shard_map/image/pallas_call | solution.py:178
  82.3 25.4 %all_to_all.37 = f32[16,8,128]{2,1,0:T(8,128)S(1)} all-to-all(f32[16,8,128]{2,1,0:T(8,128)} %image.1), channel_id=1, replica_groups=mesh['row_0'=4,'row_1'=8,'shift'=16] {'shift'}, dimensions={0} | all-to-all | bytes 131072 | tf_op jit(solution)/shard_map/all_to_all | solution.py:186
  107.8 11.0 %all_to_all.38.total = f32[16,8,128]{2,1,0:T(8,128)} all-to-all(f32[16,8,128]{2,1,0:T(8,128)S(1)} %broadcast_in_dim.19), channel_id=1, replica_groups=mesh['row_0'=4,'row_1'=8,'shift'=16] {'shift'}, dimensions={0} | all-to-all | bytes 131072 | tf_op jit(solution)/shard_map/all_to_all | solution.py:35
  118.8 7.4 %first_factor.1 = (f32[64,128]{1,0:T(8,128)}, f32[4,32,128]{2,1,0:T(8,128)}) custom-call(f32[16,8,128]{2,1,0:T(8,128)} %all_to_all.38.total), custom_call_target="tpu_custom_call" | custom-call | tf_op jit(solution)/shard_map/first_factor/pallas_call | solution.py:178
  126.2 7.7 %all_to_all.39 = f32[4,32,128]{2,1,0:T(8,128)S(1)} all-to-all(f32[4,32,128]{2,1,0:T(8,128)} %get-tuple-element.8), channel_id=1, replica_groups=mesh['row_0'=4,'row_1'=8,'shift'=16] {'row_0'}, dimensions={0} | all-to-all | bytes 131072 | tf_op jit(solution)/shard_map/all_to_all | solution.py:186
  133.9 11.1 %all_to_all.40.grams = f32[8,32,128]{2,1,0:T(8,128)} all-to-all(f32[8,32,128]{2,1,0:T(8,128)S(1)} %broadcast_in_dim.20), channel_id=1, replica_groups=mesh['row_0'=4,'row_1'=8,'shift'=16] {'row_1'}, dimensions={0} | all-to-all | bytes 262144 | tf_op jit(solution)/shard_map/all_to_all | solution.py:35
  145.0 7.2 %last_factor.1 = f32[64,128]{1,0:T(8,128)} custom-call(f32[8,32,128]{2,1,0:T(8,128)} %all_to_all.40.grams, f32[64,128]{1,0:T(8,128)} %get-tuple-element.9.mapped), custom_call_target="tpu_custom_call" | custom-call | tf_op jit(solution)/shard_map/last_factor/pallas_call | solution.py:178
  (10 shorter events, 0.1 us)
Async XLA Ops:
  0.6 0.8 copy-start.5
  0.7 0.7 copy-start.7
  1.5 33.7 %copy-start.1 = (bf16[16,8,2,128]{3,1,2,0:T(8,128)(2,1)}, bf16[16,8,2,128]{3,1,2,0:T(8,128)(2,1)S(1)}, u32[]{:S(2)}) copy-start(bf16[16,8,2,128]{3,1,2,0:T(8,128)(2,1)S(1)} %copy.16) | copy-start | bytes 196612
  1.6 15.8 %collective-permute-start = (bf16[32,256]{1,0:T(8,128)(2,1)S(1)}, bf16[32,256]{1,0:T(8,128)(2,1)S(1)}, u32[]{:S(2)}, u32[]{:S(2)}) collective-permute-start(bf16[32,256]{1,0:T(8,128)(2,1)S(1)} %fusion.2), channel_id=1, source_target_pairs={{0,256},{1,287},{2,303},{3,304},{4,320},{5,351},{6,367},{7,368},{8... | collective-permute-start | bytes 49160 | tf_op jit(solution)/shard_map/ppermute | solution.py:217
  18.2 17.6 %copy-start.6 = (bf16[128,2,128]{2,1,0:T(2,128)(2,1)S(1)}, bf16[128,2,128]{2,1,0:T(2,128)(2,1)}, u32[]{:S(2)}) copy-start(bf16[128,2,128]{2,1,0:T(2,128)(2,1)} %param.5) | copy-start | bytes 196612
  18.2 19.8 %all-to-all-start = ((bf16[32,32,256]{2,1,0:T(8,128)(2,1)}), bf16[32,32,256]{2,1,0:T(8,128)(2,1)S(1)}, u32[]{:S(2)}, u32[]{:S(2)}) async-start(bf16[32,32,256]{2,1,0:T(8,128)(2,1)} %broadcast_in_dim.17), calls=%async_computation | async-start | bytes 1048576 | tf_op jit(solution)/shard_map/all_to_all | solution.py:35
  25.5 13.2 %collective-permute-start.1 = (bf16[128,256]{1,0:T(8,128)(2,1)S(1)}, bf16[128,256]{1,0:T(8,128)(2,1)S(1)}, u32[]{:S(2)}, u32[]{:S(2)}) collective-permute-start(bf16[128,256]{1,0:T(8,128)(2,1)S(1)} %bitcast.15), channel_id=1, source_target_pairs={{0,496},{16,0},{32,16},{48,32},{64,48},{80,64},{96,80},{112,96},{1... | collective-permute-start | bytes 196616 | tf_op jit(solution)/shard_map/ppermute | solution.py:218
  32.1 10.3 %collective-permute-start.2 = (bf16[128,256]{1,0:T(8,128)(2,1)S(1)}, bf16[128,256]{1,0:T(8,128)(2,1)S(1)}, u32[]{:S(2)}, u32[]{:S(2)}) collective-permute-start(bf16[128,256]{1,0:T(8,128)(2,1)S(1)} %bitcast.16), channel_id=1, source_target_pairs={{0,496},{16,480},{32,464},{48,448},{64,432},{80,416},{96,400},{112... | collective-permute-start | bytes 196616 | tf_op jit(solution)/shard_map/ppermute | solution.py:219
  35.2 7.2 %collective-permute-start.3 = (bf16[128,256]{1,0:T(8,128)(2,1)S(1)}, bf16[128,256]{1,0:T(8,128)(2,1)S(1)}, u32[]{:S(2)}, u32[]{:S(2)}) collective-permute-start(bf16[128,256]{1,0:T(8,128)(2,1)S(1)} %bitcast.17), channel_id=1, source_target_pairs={{0,0},{16,496},{32,480},{48,464},{64,448},{80,432},{96,416},{112,4... | collective-permute-start | bytes 196616 | tf_op jit(solution)/shard_map/ppermute | solution.py:220
  38.0 4.3 %copy-start = (bf16[32,32,256]{2,1,0:T(8,128)(2,1)}, bf16[32,32,256]{2,1,0:T(8,128)(2,1)S(1)}, u32[]{:S(2)}) copy-start(bf16[32,32,256]{2,1,0:T(8,128)(2,1)S(1)} %all-to-all-done.pieces) | copy-start | bytes 1572868
  38.7 3.7 %copy-start.2 = (bf16[128,256]{1,0:T(8,128)(2,1)}, bf16[128,256]{1,0:T(8,128)(2,1)S(1)}, u32[]{:S(2)}) copy-start(bf16[128,256]{1,0:T(8,128)(2,1)S(1)} %collective-permute-done.1.after) | copy-start | bytes 196612
  42.3 0.6 copy-start.3
  42.3 0.6 copy-start.4

commit v3 on v2

--- a/solution.py
+++ b/solution.py
@@ -6,7 +6,7 @@
 from jax.sharding import Mesh
 from jax.sharding import PartitionSpec as P
 
-M = 4096
+
 K = 64
 SNAPS = 128
 SHIFTS = 48
@@ -132,16 +132,28 @@
         eye = (lane_at == row_at + (K + 8 * t)).astype(jnp.float32)
         tiles.append(jnp.where(lane_at < K, jnp.concatenate([part, part], axis=1), eye))
         done.append(jnp.zeros((8, 2 * K), jnp.float32))
-    for j in range(K):
-        at, s = divmod(j, 8)
-        row = tiles[at][s : s + 1, :]
-        cols = [jnp.broadcast_to(tiles[t][:, j : j + 1], (8, 2 * K)) for t in range(at, K // 8)]
-        pivot = cols[0][s : s + 1, :]
-        scaled = row * (1.0 / pivot)
-        done[at] = jnp.where(row_at == s, row / jnp.sqrt(pivot), done[at])
-        tiles[at] = jnp.where(row_at > s, tiles[at] - cols[0] * scaled, tiles[at])
-        for t in range(at + 1, K // 8):
-            tiles[t] = tiles[t] - cols[t - at] * scaled
+    for at in range(K // 8):
+        own, rest = at, range(at + 1, K // 8)
+        cols = [
+            [jnp.broadcast_to(tiles[t][:, j : j + 1], (8, 2 * K)) for t in range(at, K // 8)]
+            for j in range(8 * at, 8 * at + 8)
+        ]
+        for s in range(8):
+            col = cols[s]
+            below = row_at > s
+            pivot = col[0][s : s + 1, :]
+            inverse = 1.0 / pivot
+            row = tiles[own][s : s + 1, :]
+            scaled = row * inverse
+            done[own] = jnp.where(row_at == s, row / jnp.sqrt(pivot), done[own])
+            for k in range(s + 1, 8):
+                share = cols[k][0][s : s + 1, :] * inverse
+                left = [c - f * share for c, f in zip(cols[k], col)]
+                left[0] = jnp.where(below, left[0], cols[k][0])
+                cols[k] = left
+            tiles[own] = jnp.where(below, tiles[own] - col[0] * scaled, tiles[own])
+            for t in rest:
+                tiles[t] = tiles[t] - col[t - at] * scaled
     return jnp.concatenate(done, axis=0)[:, K:]
 
 
@@ -174,11 +186,9 @@
     basis[...] = dot_nn(inverse_factor(gram), mapped[...], HIGH)
 
 
-def local_call(kernel, name, shapes, *operands):
+def local_call(kernel, shapes, *operands):
     return pl.pallas_call(
-        kernel,
-        name=name,
-        out_shape=[jax.ShapeDtypeStruct(s, jnp.float32) for s in shapes],
+        kernel, out_shape=[jax.ShapeDtypeStruct(s, jnp.float32) for s in shapes]
     )(*operands)
 
 
@@ -225,13 +235,11 @@
         place, every_offset, own, after, mirror, mirror_after, tail, pieces, start_basis
     )
     mapped = total_over(mapped, ROW)
-    (terms,) = local_call(image_kernel, "image", [(16, 8, SNAPS)], mapped, cov)
+    (terms,) = local_call(image_kernel, [(16, 8, SNAPS)], mapped, cov)
     total = total_over(terms, "shift")
-    mapped, grams = local_call(
-        first_factor_kernel, "first_factor", [(K, BLOCK), (4, K // 2, 2 * K)], total
-    )
+    mapped, grams = local_call(first_factor_kernel, [(K, BLOCK), (4, K // 2, 2 * K)], total)
     grams = sent_to_all(exchanged(grams, "row_0").sum(axis=0), "row_1")
-    (basis,) = local_call(last_factor_kernel, "last_factor", [(K, BLOCK)], grams, mapped)
+    (basis,) = local_call(last_factor_kernel, [(K, BLOCK)], grams, mapped)
     return (cov, basis)
 
 

time: 153 us -> 145 us (0.948)
  Pallas kernels: 23 us -> 15.4 us
    pallas_call x3, Pallas kernels: 16.5 us -> 8.81 us  [local_call(): pl.pallas_call(kernel, out_shape=[jax.ShapeDtypeStruct(s, jnp.float32) fo...]
where the time goes in v3:
time: 145 us
  blocking collectives  86 us (59%)
  starting transfers between devices  32.5 us (22%)
  Pallas kernels  15.4 us (11%)
  waiting for transfers between devices  5.39 us (4%)
  local copies, waits for them, and re-layouts  2.95 us (2%)
    all_to_all x3, blocking collectives, exchanged(): return lax.all_to_all(tiles, axis, split_axis=0, concat_axis=0, tiled=True)  51.4 us
    all_to_all x3, blocking collectives, sent_to_all(): return lax.all_to_all(copies, axis, split_axis=0, concat_axis=0, tiled=True)  34.6 us
    ppermute x1, starting transfers between devices, per_device(): piece = lax.ppermute(piece, EVERY, piece_routes())  15 us
    pallas_call x3, Pallas kernels, local_call(): pl.pallas_call(kernel, out_shape=[jax.ShapeDtypeStruct(s, jnp.float32) fo...  8.81 us
    all_to_all x1, starting transfers between devices, sent_to_all(): return lax.all_to_all(copies, axis, split_axis=0, concat_axis=0, tiled=True)  7.28 us
    pallas_call x1, Pallas kernels, covariance_block(): pl.pallas_call(covariance_kernel, name='covariance_block', in_specs=[pl.B...  6.59 us
    ppermute x1, starting transfers between devices, per_device(): after = lax.ppermute(own, ROW, [(i, (i - 1) % 32) for i in range(32)])  6.55 us
    ppermute x1, waiting for transfers between devices, per_device(): mirror = lax.ppermute(own, ROW, [(i, 31 - i) for i in range(32)])  3.67 us
  transfers between devices with their start and end apart: 5, of which 3 were waited for; matrix products, arithmetic and copies ran while one was open for 1% of the time, Pallas kernels for 0%

profile of v3, /device:TPU:1, one launch (start us, length us, event | category | flops | bytes accessed | tf_op | source)
XLA Modules:
  0.0 144.5 jit_solution(3910902988302606522)
XLA Ops:
  0.6 0.0 copy-start.5
  0.7 0.0 copy-start.7
  0.7 0.6 copy-done.7
  1.3 0.1 copy-done.5
  1.5 0.0 copy-start.1
  1.6 15.0 %collective-permute-start = (bf16[32,256]{1,0:T(8,128)(2,1)S(1)}, bf16[32,256]{1,0:T(8,128)(2,1)S(1)}, u32[]{:S(2)}, u32[]{:S(2)}) collective-permute-start(bf16[32,256]{1,0:T(8,128)(2,1)S(1)} %fusion.2), channel_id=1, source_target_pairs={{0,256},{1,287},{2,303},{3,304},{4,320},{5,351},{6,367},{7,368},{8... | collective-permute-start | bytes 49160 | tf_op jit(solution)/shard_map/ppermute | solution.py:227
  16.5 0.8 collective-permute-done
  17.4 0.8 broadcast_in_dim.17
  18.2 0.0 copy-start.6
  18.2 7.3 %all-to-all-start = ((bf16[32,32,256]{2,1,0:T(8,128)(2,1)}), bf16[32,32,256]{2,1,0:T(8,128)(2,1)S(1)}, u32[]{:S(2)}, u32[]{:S(2)}) async-start(bf16[32,32,256]{2,1,0:T(8,128)(2,1)} %broadcast_in_dim.17), calls=%async_computation | async-start | bytes 1048576 | tf_op jit(solution)/shard_map/all_to_all | solution.py:35
  25.5 6.6 %collective-permute-start.1 = (bf16[128,256]{1,0:T(8,128)(2,1)S(1)}, bf16[128,256]{1,0:T(8,128)(2,1)S(1)}, u32[]{:S(2)}, u32[]{:S(2)}) collective-permute-start(bf16[128,256]{1,0:T(8,128)(2,1)S(1)} %bitcast.15), channel_id=1, source_target_pairs={{0,496},{16,0},{32,16},{48,32},{64,48},{80,64},{96,80},{112,96},{1... | collective-permute-start | bytes 196616 | tf_op jit(solution)/shard_map/ppermute | solution.py:228
  32.1 3.1 %collective-permute-start.2 = (bf16[128,256]{1,0:T(8,128)(2,1)S(1)}, bf16[128,256]{1,0:T(8,128)(2,1)S(1)}, u32[]{:S(2)}, u32[]{:S(2)}) collective-permute-start(bf16[128,256]{1,0:T(8,128)(2,1)S(1)} %bitcast.16), channel_id=1, source_target_pairs={{0,496},{16,480},{32,464},{48,448},{64,432},{80,416},{96,400},{112... | collective-permute-start | bytes 196616 | tf_op jit(solution)/shard_map/ppermute | solution.py:229
  35.2 0.0 copy-done.1
  35.2 0.7 collective-permute-start.3
  35.8 0.0 copy-done.6
  35.8 0.6 copy.15
  36.5 0.7 pad_add_fusion.place
  37.1 0.9 all-to-all-done.pieces
  38.0 0.0 copy-start
  38.0 0.7 slice_convert_fusion
  38.7 0.0 collective-permute-done.1.after
  38.7 0.0 copy-start.2
  38.7 3.7 %collective-permute-done.2.mirror = bf16[128,256]{1,0:T(8,128)(2,1)S(1)} collective-permute-done((bf16[128,256]{1,0:T(8,128)(2,1)S(1)}, bf16[128,256]{1,0:T(8,128)(2,1)S(1)}, u32[]{:S(2)}, u32[]{:S(2)}) %collective-permute-start.2) | collective-permute-done | bytes 65568 | tf_op jit(solution)/shard_map/ppermute | solution.py:229
  42.3 0.0 copy-start.3
  42.3 0.0 collective-permute-done.3.mirror_after
  42.3 0.0 copy-start.4
  42.3 0.0 copy-done
  42.4 0.0 copy-done.2
  42.4 0.6 copy-done.3
  43.0 0.0 copy-done.4
  43.0 6.6 %covariance_block.1 = (f32[128,256]{1,0:T(8,128)}, f32[32,4,128]{2,1,0:T(4,128)}) custom-call(s32[2]{0:T(128)} %pad_add_fusion.place, s32[16,3]{1,0:T(8,128)} %bitcast.22, bf16[128,256]{1,0:T(8,128)(2,1)} %bitcast.18, bf16[128,256]{1,0:T(8,128)(2,1)} %copy-done.2, bf16[128,256]{1,0:T(8,128)(2,1)} %copy-done.3, bf16[128,256]{1,0:T(8,128)(2,1)} %copy-done.4, ...), custom_call_target="tpu_custom_call" | custom-call | tf_op jit(solution)/shard_map/covariance_block/pallas_call | solution.py:107
  49.6 18.3 %all_to_all.35 = f32[32,4,128]{2,1,0:T(4,128)S(1)} all-to-all(f32[32,4,128]{2,1,0:T(4,128)} %get-tuple-element.7), channel_id=1, replica_groups=mesh['row_0'=4,'row_1'=8,'shift'=16] {'row_0','row_1'}, dimensions={0} | all-to-all | bytes 131072 | tf_op jit(solution)/shard_map/all_to_all | solution.py:196
  67.9 12.5 %all_to_all.36.mapped = f32[32,4,128]{2,1,0:T(4,128)} all-to-all(f32[32,4,128]{2,1,0:T(4,128)S(1)} %broadcast_in_dim.18), channel_id=1, replica_groups=mesh['row_0'=4,'row_1'=8,'shift'=16] {'row_0','row_1'}, dimensions={0} | all-to-all | bytes 131072 | tf_op jit(solution)/shard_map/all_to_all | solution.py:35
  80.5 1.9 %shard_map.59 = f32[16,8,128]{2,1,0:T(8,128)} custom-call(f32[32,4,128]{2,1,0:T(4,128)} %all_to_all.36.mapped, f32[128,256]{1,0:T(8,128)} %get-tuple-element.4.cov), custom_call_target="tpu_custom_call" | custom-call | tf_op jit(solution)/shard_map/pallas_call | solution.py:190
  82.4 25.4 %all_to_all.37 = f32[16,8,128]{2,1,0:T(8,128)S(1)} all-to-all(f32[16,8,128]{2,1,0:T(8,128)} %shard_map.59), channel_id=1, replica_groups=mesh['row_0'=4,'row_1'=8,'shift'=16] {'shift'}, dimensions={0} | all-to-all | bytes 131072 | tf_op jit(solution)/shard_map/all_to_all | solution.py:196
  107.8 11.0 %all_to_all.38.total = f32[16,8,128]{2,1,0:T(8,128)} all-to-all(f32[16,8,128]{2,1,0:T(8,128)S(1)} %broadcast_in_dim.19), channel_id=1, replica_groups=mesh['row_0'=4,'row_1'=8,'shift'=16] {'shift'}, dimensions={0} | all-to-all | bytes 131072 | tf_op jit(solution)/shard_map/all_to_all | solution.py:35
  118.8 3.6 %shard_map.60 = (f32[64,128]{1,0:T(8,128)}, f32[4,32,128]{2,1,0:T(8,128)}) custom-call(f32[16,8,128]{2,1,0:T(8,128)} %all_to_all.38.total), custom_call_target="tpu_custom_call" | custom-call | tf_op jit(solution)/shard_map/pallas_call | solution.py:190
  122.4 7.7 %all_to_all.39 = f32[4,32,128]{2,1,0:T(8,128)S(1)} all-to-all(f32[4,32,128]{2,1,0:T(8,128)} %get-tuple-element.8), channel_id=1, replica_groups=mesh['row_0'=4,'row_1'=8,'shift'=16] {'row_0'}, dimensions={0} | all-to-all | bytes 131072 | tf_op jit(solution)/shard_map/all_to_all | solution.py:196
  130.1 11.1 %all_to_all.40.grams = f32[8,32,128]{2,1,0:T(8,128)} all-to-all(f32[8,32,128]{2,1,0:T(8,128)S(1)} %broadcast_in_dim.20), channel_id=1, replica_groups=mesh['row_0'=4,'row_1'=8,'shift'=16] {'row_1'}, dimensions={0} | all-to-all | bytes 262144 | tf_op jit(solution)/shard_map/all_to_all | solution.py:35
  141.2 3.3 %shard_map.61 = f32[64,128]{1,0:T(8,128)} custom-call(f32[8,32,128]{2,1,0:T(8,128)} %all_to_all.40.grams, f32[64,128]{1,0:T(8,128)} %get-tuple-element.9.mapped), custom_call_target="tpu_custom_call" | custom-call | tf_op jit(solution)/shard_map/pallas_call | solution.py:190
  (10 shorter events, 0.1 us)
Async XLA Ops:
  0.6 0.8 copy-start.5
  0.7 0.7 copy-start.7
  1.5 33.7 %copy-start.1 = (bf16[16,8,2,128]{3,1,2,0:T(8,128)(2,1)}, bf16[16,8,2,128]{3,1,2,0:T(8,128)(2,1)S(1)}, u32[]{:S(2)}) copy-start(bf16[16,8,2,128]{3,1,2,0:T(8,128)(2,1)S(1)} %copy.16) | copy-start | bytes 196612
  1.6 15.8 %collective-permute-start = (bf16[32,256]{1,0:T(8,128)(2,1)S(1)}, bf16[32,256]{1,0:T(8,128)(2,1)S(1)}, u32[]{:S(2)}, u32[]{:S(2)}) collective-permute-start(bf16[32,256]{1,0:T(8,128)(2,1)S(1)} %fusion.2), channel_id=1, source_target_pairs={{0,256},{1,287},{2,303},{3,304},{4,320},{5,351},{6,367},{7,368},{8... | collective-permute-start | bytes 49160 | tf_op jit(solution)/shard_map/ppermute | solution.py:227
  18.2 17.6 %copy-start.6 = (bf16[128,2,128]{2,1,0:T(2,128)(2,1)S(1)}, bf16[128,2,128]{2,1,0:T(2,128)(2,1)}, u32[]{:S(2)}) copy-start(bf16[128,2,128]{2,1,0:T(2,128)(2,1)} %param.5) | copy-start | bytes 196612
  18.2 19.8 %all-to-all-start = ((bf16[32,32,256]{2,1,0:T(8,128)(2,1)}), bf16[32,32,256]{2,1,0:T(8,128)(2,1)S(1)}, u32[]{:S(2)}, u32[]{:S(2)}) async-start(bf16[32,32,256]{2,1,0:T(8,128)(2,1)} %broadcast_in_dim.17), calls=%async_computation | async-start | bytes 1048576 | tf_op jit(solution)/shard_map/all_to_all | solution.py:35
  25.5 13.2 %collective-permute-start.1 = (bf16[128,256]{1,0:T(8,128)(2,1)S(1)}, bf16[128,256]{1,0:T(8,128)(2,1)S(1)}, u32[]{:S(2)}, u32[]{:S(2)}) collective-permute-start(bf16[128,256]{1,0:T(8,128)(2,1)S(1)} %bitcast.15), channel_id=1, source_target_pairs={{0,496},{16,0},{32,16},{48,32},{64,48},{80,64},{96,80},{112,96},{1... | collective-permute-start | bytes 196616 | tf_op jit(solution)/shard_map/ppermute | solution.py:228
  32.1 10.3 %collective-permute-start.2 = (bf16[128,256]{1,0:T(8,128)(2,1)S(1)}, bf16[128,256]{1,0:T(8,128)(2,1)S(1)}, u32[]{:S(2)}, u32[]{:S(2)}) collective-permute-start(bf16[128,256]{1,0:T(8,128)(2,1)S(1)} %bitcast.16), channel_id=1, source_target_pairs={{0,496},{16,480},{32,464},{48,448},{64,432},{80,416},{96,400},{112... | collective-permute-start | bytes 196616 | tf_op jit(solution)/shard_map/ppermute | solution.py:229
  35.2 7.2 %collective-permute-start.3 = (bf16[128,256]{1,0:T(8,128)(2,1)S(1)}, bf16[128,256]{1,0:T(8,128)(2,1)S(1)}, u32[]{:S(2)}, u32[]{:S(2)}) collective-permute-start(bf16[128,256]{1,0:T(8,128)(2,1)S(1)} %bitcast.17), channel_id=1, source_target_pairs={{0,0},{16,496},{32,480},{48,464},{64,448},{80,432},{96,416},{112,4... | collective-permute-start | bytes 196616 | tf_op jit(solution)/shard_map/ppermute | solution.py:230
  38.0 4.3 %copy-start = (bf16[32,32,256]{2,1,0:T(8,128)(2,1)}, bf16[32,32,256]{2,1,0:T(8,128)(2,1)S(1)}, u32[]{:S(2)}) copy-start(bf16[32,32,256]{2,1,0:T(8,128)(2,1)S(1)} %all-to-all-done.pieces) | copy-start | bytes 1572868
  38.7 3.7 %copy-start.2 = (bf16[128,256]{1,0:T(8,128)(2,1)}, bf16[128,256]{1,0:T(8,128)(2,1)S(1)}, u32[]{:S(2)}) copy-start(bf16[128,256]{1,0:T(8,128)(2,1)S(1)} %collective-permute-done.1.after) | copy-start | bytes 196612
  42.3 0.6 copy-start.3
  42.3 0.6 copy-start.4
